TPU v7x, 32 devices: a whole 2x2x4 slice. The times are simulated.
32 devices in a mesh: tilt: 2 (over y), row: 8 (over z, x), col: 2 (over core).
Axes of the slice: x: 2, y: 2, z: 4, core: 2. Of those that a mesh axis runs over, the one named last changes fastest.
Arguments:
- object_field: float32 [2, 2048, 256], P(None, ('tilt', 'row'), 'col'), parts along dimension 1, may hold values from -4.2 to 4.2
- probe: float32 [8, 2, 128, 128], P('tilt'), parts along dimension 0, may hold values from -2.1 to 2.1
- patterns: float32 [16, 2, 2, 128, 128], P(('tilt', 'row'), 'col'), parts along dimension 0, may hold values from 0.1 to 3
- offsets: int32 [16, 2, 2, 2], P(('tilt', 'row'), 'col'), parts along dimension 0, may hold values from 0 to 256
- counts: int32 [16, 2], P(('tilt', 'row'), 'col'), parts along dimension 0, may hold values from 1 to 2, as said below
Outputs:
- object_out: float32 [2, 2048, 256], P(None, ('tilt', 'row'), 'col'), parts along dimension 1
- probe_out: float32 [8, 2, 128, 128], P('tilt'), parts along dimension 0
There are 2 independent parts, one for each index of `tilt`. A program takes and returns all parts, laid end to end along the dimension named above; each array names one. Nothing has to cross between parts.
Inputs may be any that keep to these rules, and one draw needn't show every extreme that they name: Only the first counts[r, c] slots of a tile are live; some tile has all 2 live. `offsets`: A window lies inside its tile's frame of 384 pixels a side.
All inputs are finite; a program needn't handle non-finite values.
Results may differ from a plain program's by a relative error of at most 0.0003.
Values sent between devices are 32-bit elements; how exact they have to be, the bound alone decides.
A program may use at most 64 MiB of HBM per device.

v0:
```python
import jax
import jax.numpy as jnp
from jax import lax
from jax.sharding import PartitionSpec as P

H = 128


object_rate = 1.0
probe_rate = 1.0
epsilon = 1e-06


def with_halo(block, sides, width):
    for axis, dim in sides:
        count = lax.axis_size(axis)
        forward = [(i, i + 1) for i in range(count - 1)]
        backward = [(target, source) for source, target in forward]
        low = lax.ppermute(
            lax.slice_in_dim(block, block.shape[dim] - width, None, axis=dim), axis, forward
        )
        high = lax.ppermute(lax.slice_in_dim(block, 0, width, axis=dim), axis, backward)
        block = jnp.concatenate([low, block, high], axis=dim)
    return block


def as_index(value):
    return jnp.asarray(value).astype(jnp.int32)


def dft_tables(length):
    counter = jnp.arange(length, dtype=jnp.int32)
    product = counter[:, None] * counter[None, :] % length
    angle = -2.0 * jnp.pi / length * product.astype(jnp.float32)
    norm = 1.0 / jnp.sqrt(jnp.float32(length))
    return (jnp.cos(angle) * norm, jnp.sin(angle) * norm)


def left_product(cos_table, sin_table, real_part, imag_part):
    hp = lax.Precision.HIGHEST
    real_out = jnp.einsum("ab,kbc->kac", cos_table, real_part, precision=hp) - jnp.einsum(
        "ab,kbc->kac", sin_table, imag_part, precision=hp
    )
    imag_out = jnp.einsum("ab,kbc->kac", cos_table, imag_part, precision=hp) + jnp.einsum(
        "ab,kbc->kac", sin_table, real_part, precision=hp
    )
    return (real_out, imag_out)


def right_product(real_part, imag_part, cos_table, sin_table):
    hp = lax.Precision.HIGHEST
    real_out = jnp.einsum("kab,bc->kac", real_part, cos_table, precision=hp) - jnp.einsum(
        "kab,bc->kac", imag_part, sin_table, precision=hp
    )
    imag_out = jnp.einsum("kab,bc->kac", real_part, sin_table, precision=hp) + jnp.einsum(
        "kab,bc->kac", imag_part, cos_table, precision=hp
    )
    return (real_out, imag_out)


def transform(real_part, imag_part, cos_table, sin_table):
    middle_re, middle_im = left_product(cos_table, sin_table, real_part, imag_part)
    return right_product(middle_re, middle_im, cos_table, sin_table)


def slot_terms(window, probe, pattern, cos_table, sin_table):
    window_re, window_im = (window[0], window[1])
    probe_re, probe_im = (probe[:, 0], probe[:, 1])
    exit_re = probe_re * window_re - probe_im * window_im
    exit_im = probe_re * window_im + probe_im * window_re
    far_re, far_im = transform(exit_re, exit_im, cos_table, sin_table)
    intensity = jnp.sum(far_re * far_re + far_im * far_im, axis=0)
    misfit = intensity - pattern
    back_re, back_im = transform(misfit * far_re, misfit * far_im, cos_table, -sin_table)
    grad_re = jnp.sum(probe_re * back_re + probe_im * back_im, axis=0)
    grad_im = jnp.sum(probe_re * back_im - probe_im * back_re, axis=0)
    term_re = window_re * back_re + window_im * back_im
    term_im = window_re * back_im - window_im * back_re
    return (jnp.stack([grad_re, grad_im]), jnp.stack([term_re, term_im], axis=1))


def body(object_field, probe, patterns, offsets, counts):
    width = probe.shape[-1]
    block = object_field.shape[1]
    slot_total = patterns.shape[2]
    cos_table, sin_table = dft_tables(width)
    tile_total = lax.axis_size("row") * lax.axis_size("col")
    live_count = counts[0, 0]
    frame = with_halo(object_field, (("row", 1), ("col", 2)), H)

    def slot_step(slot_index, inner):
        local_grad, probe_acc = inner
        slot_index = as_index(slot_index)
        corner_y = as_index(offsets[0, 0, slot_index, 0])
        corner_x = as_index(offsets[0, 0, slot_index, 1])
        window = lax.dynamic_slice(frame, (as_index(0), corner_y, corner_x), (2, width, width))
        window_grad, probe_term = slot_terms(
            window, probe, patterns[0, 0, slot_index], cos_table, sin_table
        )
        live = (slot_index < live_count).astype(jnp.float32)
        region = (
            lax.dynamic_slice(local_grad, (as_index(0), corner_y, corner_x), (2, width, width))
            + live * window_grad
        )
        local_grad = lax.dynamic_update_slice(local_grad, region, (as_index(0), corner_y, corner_x))
        return (local_grad, probe_acc + live * probe_term)

    start_carry = (jnp.zeros_like(frame), jnp.zeros_like(probe))
    gradient, probe_grad = lax.fori_loop(0, slot_total, slot_step, start_carry)
    upper_strip = gradient[:, :H, :]
    lower_strip = gradient[:, H + block :, :]
    middle = gradient[:, H : H + block, :]
    row_edges = jnp.concatenate([upper_strip, lower_strip], axis=1)
    row_grown = with_halo(row_edges, (("row", 1),), H)
    from_above = row_grown[:, :H, :]
    from_below = row_grown[:, 3 * H :, :]
    middle = middle.at[:, :H, :].add(from_above).at[:, block - H :, :].add(from_below)
    left_strip = middle[:, :, :H]
    right_strip = middle[:, :, H + block :]
    object_grad = middle[:, :, H : H + block]
    col_edges = jnp.concatenate([left_strip, right_strip], axis=2)
    col_grown = with_halo(col_edges, (("col", 2),), H)
    from_left = col_grown[:, :, :H]
    from_right = col_grown[:, :, 3 * H :]
    object_grad = object_grad.at[:, :, :H].add(from_left).at[:, :, block - H :].add(from_right)
    weight = (
        jnp.max(jnp.sum(probe[:, 0] * probe[:, 0] + probe[:, 1] * probe[:, 1], axis=0)) + epsilon
    )
    object_field = object_field - object_rate * object_grad / weight
    summed = lax.psum(probe_grad, ("row", "col"))
    probe = probe - probe_rate * summed / tile_total
    return (object_field, probe)


def solution(mesh):
    placed = (
        P(None, ("tilt", "row"), "col"),
        P("tilt", None, None, None),
        P(("tilt", "row"), "col", None, None, None),
        P(("tilt", "row"), "col", None, None),
        P(("tilt", "row"), "col"),
    )
    return jax.shard_map(
        body,
        mesh=mesh,
        in_specs=placed,
        out_specs=(P(None, ("tilt", "row"), "col"), P("tilt", None, None, None)),
        check_vma=False,
    )
```

profile of v0, /device:TPU:0, one launch (start us, length us, event | category | flops | bytes accessed | tf_op | source)
XLA Modules:
  0.0 179.5 jit_solution(4061278362378386647)
XLA Ops:
  7.2 4.9 %collective-permute-start = (f32[2,128,128]{2,1,0:T(8,128)}, f32[2,128,128]{2,1,0:T(8,128)S(1)}, u32[]{:S(2)}, u32[]{:S(2)}) collective-permute-start(f32[2,128,128]{2,1,0:T(8,128)} %param.23), channel_id=1, source_target_pairs={{0,2},{2,4},{4,6},{6,8},{8,10},{10,12},{12,14},{1,3},{3,5},{5,7},{... | collective-permute-start | bytes 393224 | tf_op jit(solution)/shard_map/ppermute | solution.py:19
  12.1 1.3 collective-permute-start.1
  13.4 1.7 collective-permute-done
  15.2 0.9 constant_dynamic-update-slice_fusion.1
  16.1 3.1 %collective-permute-done.1 = f32[2,128,128]{2,1,0:T(8,128)S(1)} collective-permute-done((f32[2,128,128]{2,1,0:T(8,128)}, f32[2,128,128]{2,1,0:T(8,128)S(1)}, u32[]{:S(2)}, u32[]{:S(2)}) %collective-permute-start.1) | collective-permute-done | bytes 131104 | tf_op jit(solution)/shard_map/ppermute | solution.py:22
  19.2 1.3 collective-permute-start.2
  20.5 1.3 collective-permute-start.3
  21.8 1.1 copy.41
  22.9 1.2 collective-permute-done.3
  24.1 1.1 pad_maximum_fusion
  25.3 0.8 copy-done.1
  26.1 42.4 %while.26 = (s32[]{:T(128)}, f32[2,384,384]{2,1,0:T(8,128)S(1)}, f32[4,2,128,128]{3,2,0,1:T(8,128)S(1)}, s32[1,1,2,2]{3,2,1,0:T(2,128)S(1)}, s32[]{:T(128)}, /*i...) while((s32[]{:T(128)}, f32[2,384,384]{2,1,0:T(8,128)S(1)}, ...), condition=%wide.region_4.5_spmd.clone.clone, body=%wide.region_0.4_spmd.clone.clone.sunk | while | flops 1617952768 | bytes 16646421 | solution.py:109
  30.7 1.1 dynamic-slice_bitcast_fusion.3
  31.8 0.8 fusion.238
  33.4 0.8 fusion.235
  43.0 0.8 add_bitcast_fusion.2
  44.8 2.5 %dynamic_update_slice.11 = f32[2,384,384]{2,1,0:T(8,128)S(1)} dynamic-update-slice(f32[2,384,384]{2,1,0:T(8,128)S(1)} %get-tuple-element.543, f32[2,128,128]{2,1,0:T(8,128)S(1)} %fusion.247, s32[]{:T(128)} %constant.191.clone.1..sunk, s32[]{:T(128)S(6)} %select_n.177, s32[]{:T(128)S(6)} %select_n.178) | dynamic-update-slice | bytes 262148 | tf_op jit(solution)/shard_map/while/body/eval_jaxpr/dynamic_update_slice | solution.py:105
  51.9 1.1 dynamic-slice_bitcast_fusion.3
  53.0 0.8 fusion.238
  53.8 0.8 fusion.239
  54.5 0.8 fusion.235
  64.2 0.8 add_bitcast_fusion.2
  66.0 2.5 %dynamic_update_slice.11 = f32[2,384,384]{2,1,0:T(8,128)S(1)} dynamic-update-slice(f32[2,384,384]{2,1,0:T(8,128)S(1)} %get-tuple-element.543, f32[2,128,128]{2,1,0:T(8,128)S(1)} %fusion.247, s32[]{:T(128)} %constant.191.clone.1..sunk, s32[]{:T(128)S(6)} %select_n.177, s32[]{:T(128)S(6)} %select_n.178) | dynamic-update-slice | bytes 262148 | tf_op jit(solution)/shard_map/while/body/eval_jaxpr/dynamic_update_slice | solution.py:105
  68.5 0.8 fusion.147
  69.3 4.3 %collective-permute-start.4 = (f32[2,128,384]{2,1,0:T(8,128)}, f32[2,128,384]{2,1,0:T(8,128)S(1)}, u32[]{:S(2)}, u32[]{:S(2)}) collective-permute-start(f32[2,128,384]{2,1,0:T(8,128)} %get-tuple-element.457), channel_id=1, source_target_pairs={{0,2},{2,4},{4,6},{6,8},{8,10},{10,12},{12,14},{1,3},{3,5},{5,7},{... | collective-permute-start | bytes 1179656 | tf_op jit(solution)/shard_map/ppermute | solution.py:19
  73.6 1.3 collective-permute-start.5
  76.2 0.8 copy.42
  77.1 13.5 %collective-permute-done.4 = f32[2,128,384]{2,1,0:T(8,128)S(1)} collective-permute-done((f32[2,128,384]{2,1,0:T(8,128)}, f32[2,128,384]{2,1,0:T(8,128)S(1)}, u32[]{:S(2)}, u32[]{:S(2)}) %collective-permute-start.4) | collective-permute-done | bytes 393248 | tf_op jit(solution)/shard_map/ppermute | solution.py:19
  90.7 1.4 collective-permute-start.6
  92.1 1.3 collective-permute-start.7
  93.4 76.6 %all-reduce.2.cloned.1.call-done = f32[4,2,128,128]{3,2,1,0:T(8,128)} async-done(((f32[4,2,128,128]{3,2,1,0:T(8,128)}), f32[4,2,128,128]{3,2,1,0:T(8,128)}) %all-reduce.2.cloned.1.call-update) | async-done | bytes 524304 | tf_op jit(solution)/shard_map/psum | solution.py:130
  170.0 1.9 %multiply_subtract_fusion = f32[4,2,128,128]{3,2,1,0:T(8,128)} fusion(f32[4,2,128,128]{3,2,1,0:T(8,128)S(1)} %copy-done, f32[4,2,128,128]{3,2,1,0:T(8,128)} %all-reduce.2.cloned.1.call-done), kind=kLoop, calls=%fused_computation.169 | loop fusion | flops 262144 | bytes 1572864 | tf_op jit(solution)/shard_map/sub | solution.py:131
  (55 shorter events, 21.7 us)
Async XLA Ops:
  7.2 162.9 %all-reduce.2.cloned.1.call-start = ((), (), s32[]{:S(2)}) async-start(), calls=%async_computation | async-start | bytes 1048576 | tf_op jit(solution)/shard_map/psum | solution.py:130
  7.2 7.9 %collective-permute-start = (f32[2,128,128]{2,1,0:T(8,128)}, f32[2,128,128]{2,1,0:T(8,128)S(1)}, u32[]{:S(2)}, u32[]{:S(2)}) collective-permute-start(f32[2,128,128]{2,1,0:T(8,128)} %param.23), channel_id=1, source_target_pairs={{0,2},{2,4},{4,6},{6,8},{8,10},{10,12},{12,14},{1,3},{3,5},{5,7},{... | collective-permute-start | bytes 393224 | tf_op jit(solution)/shard_map/ppermute | solution.py:19
  12.1 7.1 %collective-permute-start.1 = (f32[2,128,128]{2,1,0:T(8,128)}, f32[2,128,128]{2,1,0:T(8,128)S(1)}, u32[]{:S(2)}, u32[]{:S(2)}) collective-permute-start(f32[2,128,128]{2,1,0:T(8,128)} %param.23), channel_id=1, source_target_pairs={{2,0},{4,2},{6,4},{8,6},{10,8},{12,10},{14,12},{3,1},{5,3},{7,5},{... | collective-permute-start | bytes 393224 | tf_op jit(solution)/shard_map/ppermute | solution.py:22
  19.2 3.7 %collective-permute-start.2 = (f32[2,384,128]{2,1,0:T(8,128)S(1)}, f32[2,384,128]{2,1,0:T(8,128)S(1)}, u32[]{:S(2)}, u32[]{:S(2)}) collective-permute-start(f32[2,384,128]{2,1,0:T(8,128)S(1)} %constant_dynamic-update-slice_fusion), channel_id=1, source_target_pairs={{0,1},{2,3},{4,5},{6,7},{8,9},{10,11},{12,13},{14,15},{16,17},{18,... | collective-permute-start | bytes 1179656 | tf_op jit(solution)/shard_map/ppermute | solution.py:19
  20.5 3.6 %collective-permute-start.3 = (f32[2,384,128]{2,1,0:T(8,128)S(1)}, f32[2,384,128]{2,1,0:T(8,128)S(1)}, u32[]{:S(2)}, u32[]{:S(2)}) collective-permute-start(f32[2,384,128]{2,1,0:T(8,128)S(1)} %constant_dynamic-update-slice_fusion), channel_id=1, source_target_pairs={{1,0},{3,2},{5,4},{7,6},{9,8},{11,10},{13,12},{15,14},{17,16},{19,... | collective-permute-start | bytes 1179656 | tf_op jit(solution)/shard_map/ppermute | solution.py:22
  25.2 0.9 copy-start.1
  25.2 0.9 copy-start.3
  68.5 6.4 %copy-start = (f32[4,2,128,128]{3,2,1,0:T(8,128)S(1)}, f32[4,2,128,128]{3,2,1,0:T(8,128)}, u32[]{:S(2)}) copy-start(f32[4,2,128,128]{3,2,1,0:T(8,128)} %param.24) | copy-start | bytes 1572868
  69.3 21.3 %collective-permute-start.4 = (f32[2,128,384]{2,1,0:T(8,128)}, f32[2,128,384]{2,1,0:T(8,128)S(1)}, u32[]{:S(2)}, u32[]{:S(2)}) collective-permute-start(f32[2,128,384]{2,1,0:T(8,128)} %get-tuple-element.457), channel_id=1, source_target_pairs={{0,2},{2,4},{4,6},{6,8},{8,10},{10,12},{12,14},{1,3},{3,5},{5,7},{... | collective-permute-start | bytes 1179656 | tf_op jit(solution)/shard_map/ppermute | solution.py:19
  73.6 16.9 %collective-permute-start.5 = (f32[2,128,384]{2,1,0:T(8,128)S(1)}, f32[2,128,384]{2,1,0:T(8,128)S(1)}, u32[]{:S(2)}, u32[]{:S(2)}) collective-permute-start(f32[2,128,384]{2,1,0:T(8,128)S(1)} %get-tuple-element.458), channel_id=1, source_target_pairs={{2,0},{4,2},{6,4},{8,6},{10,8},{12,10},{14,12},{3,1},{5,3},{7,5},{... | collective-permute-start | bytes 1179656 | tf_op jit(solution)/shard_map/ppermute | solution.py:22
  90.6 81.3 %copy-start.2 = (f32[2,128,128]{2,1,0:T(8,128)S(1)}, f32[2,128,128]{2,1,0:T(8,128)}, u32[]{:S(2)}) copy-start(f32[2,128,128]{2,1,0:T(8,128)} %param.23) | copy-start | bytes 393220
  90.7 81.3 %collective-permute-start.6 = (f32[2,128,128]{2,1,0:T(8,128)S(1)}, f32[2,128,128]{2,1,0:T(8,128)S(1)}, u32[]{:S(2)}, u32[]{:S(2)}) collective-permute-start(f32[2,128,128]{2,1,0:T(8,128)S(1)} %get-tuple-element.459), channel_id=1, source_target_pairs={{0,1},{2,3},{4,5},{6,7},{8,9},{10,11},{12,13},{14,15},{16,17},{18,... | collective-permute-start | bytes 393224 | tf_op jit(solution)/shard_map/ppermute | solution.py:19
  92.1 79.8 %collective-permute-start.7 = (f32[2,128,128]{2,1,0:T(8,128)S(1)}, f32[2,128,128]{2,1,0:T(8,128)S(1)}, u32[]{:S(2)}, u32[]{:S(2)}) collective-permute-start(f32[2,128,128]{2,1,0:T(8,128)S(1)} %get-tuple-element.460), channel_id=1, source_target_pairs={{1,0},{3,2},{5,4},{7,6},{9,8},{11,10},{13,12},{15,14},{17,16},{19,... | collective-permute-start | bytes 393224 | tf_op jit(solution)/shard_map/ppermute | solution.py:22
Sparse Core Ops, SparseCore 0:
  77.2 92.7 all-reduce.1
where the time goes:
time: 180 us; the launch traced here: 179 us
  waiting for transfers between devices  96.2 us (53%)
  matrix products  23.8 us (13%)
  starting transfers between devices  17.1 us (10%)
  between operations  14.8 us (8%)
  local copies, waits for them, and re-layouts  12.9 us (7%)
  loops' own time  9.63 us (5%)
  other arithmetic  4.97 us (3%)
    psum x1, waiting for transfers between devices, body(): summed = lax.psum(probe_grad, ('row', 'col'))  76.6 us
    ppermute x4, waiting for transfers between devices, with_halo(): lax.ppermute(lax.slice_in_dim(block, block.shape[dim] - width, None, axis...  15.2 us
    ppermute x4, starting transfers between devices, with_halo(): lax.ppermute(lax.slice_in_dim(block, block.shape[dim] - width, None, axis...  11.9 us
    another operation x1, loops' own time, body(): gradient, probe_grad = lax.fori_loop(0, slot_total, slot_step, start_carry)  9.63 us
    ppermute x4, starting transfers between devices, with_halo(): lax.ppermute(lax.slice_in_dim(block, 0, width, axis=dim), axis, backward)  5.17 us
    dynamic_update_slice x2, local copies, waits for them, and re-layouts, slot_step(): lax.dynamic_update_slice(local_grad, region, (as_index(0), corner_y, corn...  4.99 us
    ppermute x4, waiting for transfers between devices, with_halo(): lax.ppermute(lax.slice_in_dim(block, 0, width, axis=dim), axis, backward)  4.31 us
  transfers between devices with their start and end apart: 9, of which 5 were waited for; matrix products, arithmetic and copies ran while one was open for 3% of the time, Pallas kernels for 0%

commit v1 on v0

v1 whole, which is shorter than its diff:
```python
import functools

import jax
import jax.numpy as jnp
import numpy as np
from jax import lax
from jax.experimental import pallas as pl
from jax.experimental.pallas import tpu as pltpu
from jax.sharding import PartitionSpec as P

MESH = pl.DeviceIdType.MESH
F32 = jnp.float32
BF16 = jnp.bfloat16

object_rate = 1.0
probe_rate = 1.0
epsilon = 1e-06


def split_table(table):
    high = table.astype(jnp.bfloat16)
    low = (table - high.astype(np.float64)).astype(jnp.bfloat16)
    return high, low


def dft_tables(length):
    counter = np.arange(length)
    product = counter[:, None] * counter[None, :] % length
    angle = -2.0 * np.pi / length * product
    c, s = np.cos(angle) / np.sqrt(length), np.sin(angle) / np.sqrt(length)
    right = np.block([[c, s], [-s, c]])
    left = right.T
    return np.stack([*split_table(right), *split_table(left)])


def split(x):
    high = x.astype(BF16)
    return high, (x - high.astype(F32)).astype(BF16)


def each_peer(total, step):
    if total <= 16:
        for hop in range(1, total):
            step(hop)
    else:
        lax.fori_loop(1, total, lambda hop, carry: (step(hop), carry)[1], 0)


def dot(a, b):
    return jnp.dot(a, b, preferred_element_type=F32)


def kernel(
    rows, modes, slots, width, owners,
    off_ref, cnt_ref, obj_ref, probe_ref, pat_ref, tab_ref,
    obj_out, probe_out,
    frame, xh, xl, yh, yl, far, vh, vl, win, gacc,
    gown, gpar, grecv, gedge, term, tpart, acc, pieces, red, red_other,
    h_send, h_recv, g_send, g_recv, e_send, e_recv, t_send, t_recv,
    rs_send, rs_recv, ag_send, ag_recv, o_send, o_recv,
):
    me = lax.axis_index("row")
    col = lax.axis_index("col")
    n = width
    tiles = rows * 2
    mate = {"col": 1 - col}
    up = {"row": me - 1}
    down = {"row": me + 1}
    has_up, has_down = me > 0, me < rows - 1
    chunk = 2 * n // owners

    barrier = pltpu.get_barrier_semaphore()
    pl.semaphore_signal(barrier, inc=1, device_id=mate, device_id_type=MESH)

    def greet(hop):
        other = lax.rem(me + hop, rows)
        pl.semaphore_signal(barrier, inc=1, device_id={"row": other}, device_id_type=MESH)

    each_peer(rows, greet)
    pl.semaphore_wait(barrier, rows)

    def remote(src, dst, send, recv, to):
        return pltpu.make_async_remote_copy(
            src_ref=src, dst_ref=dst, send_sem=send, recv_sem=recv, device_id=to, device_id_type=MESH
        )

    seen = 2 * col
    mine = 2 - 2 * col
    to_mate = remote(obj_ref, frame.at[1, seen], h_send.at[0], h_recv.at[0], mate)
    to_up = remote(obj_ref, frame.at[2, 1], h_send.at[1], h_recv.at[2], up)
    to_down = remote(obj_ref, frame.at[0, 1], h_send.at[2], h_recv.at[1], down)
    relay_up = remote(frame.at[0, 1], frame.at[0, seen], h_send.at[3], h_recv.at[3], mate)
    relay_down = remote(frame.at[2, 1], frame.at[2, seen], h_send.at[4], h_recv.at[4], mate)
    pl.when(has_up)(to_up.start)
    pl.when(has_down)(to_down.start)
    to_mate.start()

    zero = jnp.zeros((2, n, n), F32)
    frame[1, 1] = obj_ref[...]
    for j in range(3):
        frame[j, seen] = zero

    @pl.when(me == 0)
    def _():
        frame[0, 1] = zero
        frame[0, mine] = zero

    @pl.when(me == rows - 1)
    def _():
        frame[2, 1] = zero
        frame[2, mine] = zero

    power = jnp.zeros((n, n), F32)
    for k in range(modes):
        power = power + (probe_ref[k, 0] * probe_ref[k, 0] + probe_ref[k, 1] * probe_ref[k, 1])
    weight = jnp.max(power) + epsilon

    @pl.when(has_up)
    def _():
        to_down.wait_recv()
        relay_up.start()

    @pl.when(has_down)
    def _():
        to_up.wait_recv()
        relay_down.start()

    to_mate.wait_recv()
    pl.when(has_up)(relay_up.wait_recv)
    pl.when(has_down)(relay_down.wait_recv)

    r_hi, r_lo, l_hi, l_lo = (tab_ref.at[t] for t in range(4))
    row_id = lax.broadcasted_iota(jnp.int32, (n, n), 0)
    lane_id = lax.broadcasted_iota(jnp.int32, (n, n), 1)

    def place(s):
        oy, ox = off_ref[0, 0, s, 0], off_ref[0, 0, s, 1]
        by, bx = oy // n, ox // n
        return by, bx, oy - by * n, ox - bx * n

    for s in range(slots):
        by, bx, sy, sx = place(s)
        by2, bx2 = jnp.minimum(by + 1, 2), jnp.minimum(bx + 1, 2)
        for q in range(2):
            upper = jnp.where(lane_id >= sx, frame[by, bx, q], frame[by, bx2, q])
            lower = jnp.where(lane_id >= sx, frame[by2, bx, q], frame[by2, bx2, q])
            packed = jnp.where(row_id >= sy, upper, lower)
            packed = pltpu.roll(packed, lax.rem(n - sy, n), 0)
            win[s, q] = pltpu.roll(packed, lax.rem(n - sx, n), 1)
        for k in range(modes):
            wr, wi = win[s, 0], win[s, 1]
            pr, pi = probe_ref[k, 0], probe_ref[k, 1]
            for q, part in enumerate((pr * wr - pi * wi, pr * wi + pi * wr)):
                hi, lo = split(part)
                xh[s, k * n : (k + 1) * n, q * n : (q + 1) * n] = hi
                xl[s, k * n : (k + 1) * n, q * n : (q + 1) * n] = lo
        for k in range(modes):
            a_hi, a_lo = xh[s, k * n : (k + 1) * n, :], xl[s, k * n : (k + 1) * n, :]
            y = dot(a_hi, r_hi[...]) + dot(a_lo, r_hi[...]) + dot(a_hi, r_lo[...])
            for q in range(2):
                hi, lo = split(y[:, q * n : (q + 1) * n])
                yh[s, q * n : (q + 1) * n, k * n : (k + 1) * n] = hi
                yl[s, q * n : (q + 1) * n, k * n : (k + 1) * n] = lo
        for p in range(modes // 2):
            cols = slice(2 * p * n, 2 * (p + 1) * n)
            b_hi, b_lo = yh[s, :, cols], yl[s, :, cols]
            far[s, :, cols] = dot(l_hi[...], b_hi) + dot(l_lo[...], b_hi) + dot(l_hi[...], b_lo)
        level = jnp.zeros((n, n), F32)
        for k in range(modes):
            cols = slice(k * n, (k + 1) * n)
            level = level + far[s, :n, cols] * far[s, :n, cols] + far[s, n:, cols] * far[s, n:, cols]
        live = (s < cnt_ref[0, 0]).astype(F32)
        misfit = live * (level - pat_ref[0, 0, s])
        for k in range(modes):
            for q in range(2):
                spot = (s, slice(q * n, (q + 1) * n), slice(k * n, (k + 1) * n))
                hi, lo = split(misfit * far[spot])
                yh[spot] = hi
                yl[spot] = lo

    def to_partner(p):
        return remote(term.at[2 * p + 1 - col], tpart.at[p], t_send.at[p], t_recv.at[p], mate)

    for p in range(modes // 2):
        cols = slice(2 * p * n, 2 * (p + 1) * n)
        for s in range(slots):
            b_hi, b_lo = yh[s, :, cols], yl[s, :, cols]
            v = dot(r_hi[...], b_hi) + dot(r_lo[...], b_hi) + dot(r_hi[...], b_lo)
            for m in range(2):
                for q in range(2):
                    hi, lo = split(v[q * n : (q + 1) * n, m * n : (m + 1) * n])
                    vh[s, m * n : (m + 1) * n, q * n : (q + 1) * n] = hi
                    vl[s, m * n : (m + 1) * n, q * n : (q + 1) * n] = lo
            for m in range(2):
                k = 2 * p + m
                a_hi, a_lo = vh[s, m * n : (m + 1) * n, :], vl[s, m * n : (m + 1) * n, :]
                back = dot(a_hi, l_hi[...]) + dot(a_lo, l_hi[...]) + dot(a_hi, l_lo[...])
                br, bi = back[:, :n], back[:, n:]
                pr, pi = probe_ref[k, 0], probe_ref[k, 1]
                gr, gi = pr * br + pi * bi, pr * bi - pi * br
                wr, wi = win[s, 0], win[s, 1]
                tr, ti = wr * br + wi * bi, wr * bi - wi * br
                if k == 0:
                    gacc[s, 0], gacc[s, 1] = gr, gi
                else:
                    gacc[s, 0], gacc[s, 1] = gacc[s, 0] + gr, gacc[s, 1] + gi
                if s == 0:
                    term[k, 0], term[k, 1] = tr, ti
                else:
                    term[k, 0], term[k, 1] = term[k, 0] + tr, term[k, 1] + ti
        to_partner(p).start()

    for q in range(2):
        own = [jnp.zeros((n, n), F32)] * 3
        par = [jnp.zeros((n, n), F32)] * 3
        for s in range(slots):
            by, bx, sy, sx = place(s)
            g = pltpu.roll(pltpu.roll(gacc[s, q], sy, 0), sx, 1)
            low_x, low_y = (lane_id >= sx).astype(F32), (row_id >= sy).astype(F32)

            def side(block, at, low):
                return (block == at).astype(F32) * low + (block == at + 1).astype(F32) * (1.0 - low)

            g_own, g_par = g * side(1, bx, low_x), g * side(mine, bx, low_x)
            for j in range(3):
                mask = side(j, by, low_y)
                own[j] = own[j] + g_own * mask
                par[j] = par[j] + g_par * mask
        for j in range(3):
            gown[j, q] = own[j]
            gpar[j, q] = par[j]
    across = remote(gpar, grecv, g_send.at[0], g_recv.at[0], mate)
    across.start()

    def row_slice(ref, p, owner):
        return ref.at[p, pl.ds(pl.multiple_of(owner * chunk, 8), chunk)]

    def scatter(p, hop):
        to = lax.rem(me + hop, rows)
        src = lax.rem(me + rows - hop, rows)
        return (
            to,
            remote(row_slice(acc, p, to), pieces.at[p, hop], rs_send.at[p, hop], rs_recv.at[p, hop], {"row": to}),
        )

    def start_scatter(p):
        to_partner(p).wait()
        for q in range(2):
            acc[p, q * n : (q + 1) * n] = term[2 * p + col, q] + tpart[p, q]

        def step(hop):
            to, copy = scatter(p, hop)
            pl.when(to < owners)(copy.start)

        each_peer(rows, step)

    start_scatter(0)

    across.wait()
    for j in range(3):
        gown[j] = gown[j] + grecv[j]
    edge_up = remote(gown.at[0], gedge.at[1], e_send.at[0], e_recv.at[1], up)
    edge_down = remote(gown.at[2], gedge.at[0], e_send.at[1], e_recv.at[0], down)
    pl.when(has_up)(edge_up.start)
    pl.when(has_down)(edge_down.start)

    for p in range(1, modes // 2):
        start_scatter(p)

    def gather(p, hop):
        to = lax.rem(me + hop, rows)
        here = row_slice(red, p, me)
        return remote(here, here, ag_send.at[p, hop], ag_recv.at[p, hop], {"row": to})

    for p in range(modes // 2):

        @pl.when(me < owners)
        def _():
            red_chunk = row_slice(acc, p, me)[...]

            if rows <= 16:
                for hop in range(1, rows):
                    scatter(p, hop)[1].wait_recv()
                    red_chunk = red_chunk + pieces[p, hop]
            else:

                def add(hop, total):
                    scatter(p, hop)[1].wait_recv()
                    return total + pieces[p, hop]

                red_chunk = lax.fori_loop(1, rows, add, red_chunk)
            row_slice(red, p, me)[...] = red_chunk
            each_peer(rows, lambda hop: gather(p, hop).start())

    @pl.when(jnp.logical_not(has_up))
    def _():
        gedge[0] = zero

    @pl.when(jnp.logical_not(has_down))
    def _():
        gedge[1] = zero

    pl.when(has_up)(edge_down.wait_recv)
    pl.when(has_down)(edge_up.wait_recv)
    for q in range(2):
        grad = gown[1, q] + gedge[0, q] + gedge[1, q]
        obj_out[q] = obj_ref[q] - object_rate * grad / weight

    def swap(p):
        return remote(red.at[p], red_other.at[p], o_send.at[p], o_recv.at[p], mate)

    for p in range(modes // 2):

        def step(hop):
            src = lax.rem(me + rows - hop, rows)
            pl.when(src < owners)(gather(p, hop).wait_recv)

        each_peer(rows, step)
        swap(p).start()
        k = 2 * p + col
        for q in range(2):
            probe_out[k, q] = probe_ref[k, q] - probe_rate * red[p, q * n : (q + 1) * n] / tiles
    for p in range(modes // 2):
        swap(p).wait()
        k = 2 * p + 1 - col
        for q in range(2):
            probe_out[k, q] = probe_ref[k, q] - probe_rate * red_other[p, q * n : (q + 1) * n] / tiles

    to_mate.wait_send()

    @pl.when(has_up)
    def _():
        to_up.wait_send()
        relay_up.wait_send()
        edge_up.wait_send()

    @pl.when(has_down)
    def _():
        to_down.wait_send()
        relay_down.wait_send()
        edge_down.wait_send()

    for p in range(modes // 2):

        def drain(hop):
            to, copy = scatter(p, hop)
            pl.when(to < owners)(copy.wait_send)
            pl.when(me < owners)(gather(p, hop).wait_send)

        each_peer(rows, drain)


def body(rows, object_field, probe, patterns, offsets, counts):
    modes, _, n, _ = probe.shape
    slots = patterns.shape[2]
    pairs = modes // 2
    owners = min(rows, 2 * n // 8)
    tables = jnp.asarray(dft_tables(n))
    vmem = pl.BlockSpec(memory_space=pltpu.VMEM)
    smem = pl.BlockSpec(memory_space=pltpu.SMEM)
    dma = pltpu.SemaphoreType.DMA
    wide, tall = (slots, 2 * n, modes * n), (slots, modes * n, 2 * n)
    return pl.pallas_call(
        functools.partial(kernel, rows, modes, slots, n, owners),
        out_shape=(
            jax.ShapeDtypeStruct(object_field.shape, F32),
            jax.ShapeDtypeStruct(probe.shape, F32),
        ),
        in_specs=[smem, smem, vmem, vmem, vmem, vmem],
        out_specs=(vmem, vmem),
        scratch_shapes=[
            pltpu.VMEM((3, 3, 2, n, n), F32),
            pltpu.VMEM(tall, BF16),
            pltpu.VMEM(tall, BF16),
            pltpu.VMEM(wide, BF16),
            pltpu.VMEM(wide, BF16),
            pltpu.VMEM(wide, F32),
            pltpu.VMEM((slots, 2 * n, 2 * n), BF16),
            pltpu.VMEM((slots, 2 * n, 2 * n), BF16),
            pltpu.VMEM((slots, 2, n, n), F32),
            pltpu.VMEM((slots, 2, n, n), F32),
            pltpu.VMEM((3, 2, n, n), F32),
            pltpu.VMEM((3, 2, n, n), F32),
            pltpu.VMEM((3, 2, n, n), F32),
            pltpu.VMEM((2, 2, n, n), F32),
            pltpu.VMEM((modes, 2, n, n), F32),
            pltpu.VMEM((pairs, 2, n, n), F32),
            pltpu.VMEM((pairs, 2 * n, n), F32),
            pltpu.VMEM((pairs, rows, 2 * n // owners, n), F32),
            pltpu.VMEM((pairs, 2 * n, n), F32),
            pltpu.VMEM((pairs, 2 * n, n), F32),
            dma((5,)), dma((5,)), dma((1,)), dma((1,)), dma((2,)), dma((2,)),
            dma((pairs,)), dma((pairs,)),
            dma((pairs, rows)), dma((pairs, rows)), dma((pairs, rows)), dma((pairs, rows)),
            dma((pairs,)), dma((pairs,)),
        ],
        compiler_params=pltpu.CompilerParams(collective_id=0, has_side_effects=True),
    )(offsets, counts, object_field, probe, patterns, tables)


def solution(mesh):
    placed = (
        P(None, ("tilt", "row"), "col"),
        P("tilt", None, None, None),
        P(("tilt", "row"), "col", None, None, None),
        P(("tilt", "row"), "col", None, None),
        P(("tilt", "row"), "col"),
    )
    return jax.shard_map(
        functools.partial(body, mesh.shape["row"]),
        mesh=mesh,
        in_specs=placed,
        out_specs=(P(None, ("tilt", "row"), "col"), P("tilt", None, None, None)),
        check_vma=False,
    )
```

time: 180 us -> 42 us (0.23)
  waiting for transfers between devices: 96.2 us -> 0 us
  Pallas kernels: 0 us -> 37 us
  matrix products: 23.8 us -> 0 us
  starting transfers between devices: 17.1 us -> 0 us
  between operations: 14.8 us -> 1.29 us
  loops' own time: 9.63 us -> 0 us
  local copies, waits for them, and re-layouts: 12.9 us -> 3.44 us
  other arithmetic: 4.97 us -> 0 us
    psum x1 -> x0, waiting for transfers between devices: 76.6 us -> none  [body(): summed = lax.psum(probe_grad, ('row', 'col'))]
    pallas_call x0 -> x1, Pallas kernels: none -> 37 us  [body(): pl.pallas_call(functools.partial(kernel, rows, modes, slots, n, owners),...]
    dot_general x32 -> x0, matrix products: 23.8 us -> none  [the longest x4 3.06 us: right_product(): jnp.einsum('kab,bc->kac', imag_part, sin_table, precision=hp)]
    ppermute x8 -> x0, waiting for transfers between devices: 19.5 us -> none  [the longest x4 15.2 us: with_halo(): lax.ppermute(lax.slice_in_dim(block, block.shape[dim] - width, None, axis...]
    ppermute x8 -> x0, starting transfers between devices: 17.1 us -> none  [the longest x4 11.9 us: with_halo(): lax.ppermute(lax.slice_in_dim(block, block.shape[dim] - width, None, axis...]
    another operation x1 -> x0, loops' own time: 9.63 us -> none  [body(): gradient, probe_grad = lax.fori_loop(0, slot_total, slot_step, start_carry)]
    dynamic_update_slice x2 -> x0, local copies, waits for them, and re-layouts: 4.99 us -> none  [slot_step(): lax.dynamic_update_slice(local_grad, region, (as_index(0), corner_y, corn...]
    sub x4 -> x0, other arithmetic: 2.61 us -> none  [the longest x1 1.89 us: body(): probe = probe - probe_rate * summed / tile_total]
  transfers between devices with their start and end apart: 9 -> 0, of which waited for: 5 -> 0; matrix products, arithmetic and copies ran while one was open for 3% -> 0% of each run, Pallas kernels for 0% -> 0%
where the time goes in v1:
time: 42 us; the launch traced here: 41.7 us
  Pallas kernels  37 us (88%)
  local copies, waits for them, and re-layouts  3.44 us (8%)
  between operations  1.29 us (3%)
    pallas_call x1, Pallas kernels, body(): pl.pallas_call(functools.partial(kernel, rows, modes, slots, n, owners),...  37 us
    unnamed x2, local copies, waits for them, and re-layouts  3.44 us

profile of v1, /device:TPU:0, one launch (start us, length us, event | category | flops | bytes accessed | tf_op | source)
XLA Modules:
  0.0 41.7 jit_solution(4882715475710211540)
XLA Ops:
  1.3 37.0 %shard_map.77 = (f32[2,128,128]{2,1,0:T(8,128)}, f32[4,2,128,128]{3,2,1,0:T(8,128)}) custom-call(s32[1,1,2,2]{3,2,1,0:T(2,128)} %off_ref.1, s32[1,1]{1,0:T(1,128)S(6)} %copy.10.cnt_ref, f32[2,128,128]{2,1,0:T(8,128)} %obj_ref.1, f32[4,2,128,128]{3,2,1,0:T(8,128)} %probe_ref.1, f32[1,1,2,128,128]{4,3,2,1,0:T(8,128)} %pat_ref.1, ...), custom_call_target="tpu_custom_call" | custom-call | tf_op jit(solution)/shard_map/pallas_call | solution.py:363
  38.3 1.6 %copy.11 = f32[2,128,128]{2,1,0:T(8,128)} copy(f32[2,128,128]{2,1,0:T(8,128)} %get-tuple-element.4) | data formatting | bytes 262144
  39.9 1.9 %copy.12 = f32[4,2,128,128]{3,2,1,0:T(8,128)} copy(f32[4,2,128,128]{3,2,1,0:T(8,128)} %get-tuple-element.5) | data formatting | bytes 1048576

commit v2 on v1

--- a/solution.py
+++ b/solution.py
@@ -57,27 +57,50 @@
     frame, xh, xl, yh, yl, far, vh, vl, win, gacc,
     gown, gpar, grecv, gedge, term, tpart, acc, pieces, red, red_other,
     h_send, h_recv, g_send, g_recv, e_send, e_recv, t_send, t_recv,
-    rs_send, rs_recv, ag_send, ag_recv, o_send, o_recv,
+    rs_send, rs_recv, ag_send, ag_recv, o_send, o_recv, news,
 ):
     me = lax.axis_index("row")
     col = lax.axis_index("col")
     n = width
     tiles = rows * 2
     mate = {"col": 1 - col}
-    up = {"row": me - 1}
-    down = {"row": me + 1}
-    has_up, has_down = me > 0, me < rows - 1
+    odd = lax.rem(me, 2)
+    pair = {"row": me + 1 - 2 * odd}
+    ahead, behind = me + 2 - 4 * odd, me - 2 + 4 * odd
+    has_ahead = jnp.logical_and(ahead >= 0, ahead < rows)
+    has_behind = jnp.logical_and(behind >= 0, behind < rows)
     chunk = 2 * n // owners
 
+    def if_row(row, act):
+        pl.when(jnp.logical_and(row >= 0, row < rows))(lambda: act({"row": row}))
+
+    def present(distance):
+        return (me >= distance).astype(jnp.int32) + (me + distance < rows).astype(jnp.int32)
+
     barrier = pltpu.get_barrier_semaphore()
-    pl.semaphore_signal(barrier, inc=1, device_id=mate, device_id_type=MESH)
-
-    def greet(hop):
-        other = lax.rem(me + hop, rows)
-        pl.semaphore_signal(barrier, inc=1, device_id={"row": other}, device_id_type=MESH)
-
-    each_peer(rows, greet)
-    pl.semaphore_wait(barrier, rows)
+
+    def greet(to):
+        pl.semaphore_signal(barrier, inc=1, device_id=to, device_id_type=MESH)
+
+    greet(mate)
+    greet(pair)
+    if_row(me - 2, greet)
+    if_row(me + 2, greet)
+    pl.semaphore_wait(barrier, 2 + present(2))
+
+    rounds = [2]
+    while 2 * rounds[-1] < rows:
+        rounds.append(2 * rounds[-1])
+
+    def tell(r):
+        def act(to):
+            pl.semaphore_signal(news.at[r], inc=1, device_id=to, device_id_type=MESH)
+
+        if_row(me - rounds[r], act)
+        if_row(me + rounds[r], act)
+
+    def hear(r):
+        pl.semaphore_wait(news.at[r], present(rounds[r]))
 
     def remote(src, dst, send, recv, to):
         return pltpu.make_async_remote_copy(
@@ -86,48 +109,54 @@
 
     seen = 2 * col
     mine = 2 - 2 * col
+    pj, fj = 2 - 2 * odd, 2 * odd
     to_mate = remote(obj_ref, frame.at[1, seen], h_send.at[0], h_recv.at[0], mate)
-    to_up = remote(obj_ref, frame.at[2, 1], h_send.at[1], h_recv.at[2], up)
-    to_down = remote(obj_ref, frame.at[0, 1], h_send.at[2], h_recv.at[1], down)
-    relay_up = remote(frame.at[0, 1], frame.at[0, seen], h_send.at[3], h_recv.at[3], mate)
-    relay_down = remote(frame.at[2, 1], frame.at[2, seen], h_send.at[4], h_recv.at[4], mate)
-    pl.when(has_up)(to_up.start)
-    pl.when(has_down)(to_down.start)
+    swaps, hops, relays, passes = [], [], [], []
+    for q in range(2):
+        swaps.append(remote(obj_ref.at[q], frame.at[fj, 1, q], h_send.at[1 + q], h_recv.at[1 + q], pair))
+        hops.append(remote(frame.at[pj, 1, q], frame.at[fj, 1, q], h_send.at[3 + q], h_recv.at[3 + q], {"row": ahead}))
+        relays.append(remote(frame.at[pj, 1, q], frame.at[pj, seen, q], h_send.at[5 + q], h_recv.at[5 + q], mate))
+        passes.append(remote(frame.at[fj, 1, q], frame.at[fj, seen, q], h_send.at[7 + q], h_recv.at[7 + q], mate))
+    for q in range(2):
+        swaps[q].start()
     to_mate.start()
+    tell(0)
 
     zero = jnp.zeros((2, n, n), F32)
     frame[1, 1] = obj_ref[...]
     for j in range(3):
         frame[j, seen] = zero
 
-    @pl.when(me == 0)
+    @pl.when(jnp.logical_not(has_behind))
     def _():
-        frame[0, 1] = zero
-        frame[0, mine] = zero
-
-    @pl.when(me == rows - 1)
-    def _():
-        frame[2, 1] = zero
-        frame[2, mine] = zero
+        frame[fj, 1] = zero
+        frame[fj, mine] = zero
 
     power = jnp.zeros((n, n), F32)
     for k in range(modes):
         power = power + (probe_ref[k, 0] * probe_ref[k, 0] + probe_ref[k, 1] * probe_ref[k, 1])
     weight = jnp.max(power) + epsilon
 
-    @pl.when(has_up)
-    def _():
-        to_down.wait_recv()
-        relay_up.start()
-
-    @pl.when(has_down)
-    def _():
-        to_up.wait_recv()
-        relay_down.start()
+    for q in range(2):
+        swaps[q].wait_recv()
+        pl.when(has_ahead)(hops[q].start)
+        relays[q].start()
+    for q in range(2):
+
+        @pl.when(has_behind)
+        def _():
+            hops[q].wait_recv()
+            passes[q].start()
 
     to_mate.wait_recv()
-    pl.when(has_up)(relay_up.wait_recv)
-    pl.when(has_down)(relay_down.wait_recv)
+    for q in range(2):
+        relays[q].wait_recv()
+        pl.when(has_behind)(passes[q].wait_recv)
+    for r in range(len(rounds)):
+        if r:
+            tell(r)
+        if r == 0 or r < len(rounds) - 1:
+            hear(r)
 
     r_hi, r_lo, l_hi, l_lo = (tab_ref.at[t] for t in range(4))
     row_id = lax.broadcasted_iota(jnp.int32, (n, n), 0)
@@ -254,18 +283,26 @@
 
         each_peer(rows, step)
 
+    if len(rounds) > 1:
+        hear(len(rounds) - 1)
     start_scatter(0)
 
     across.wait()
     for j in range(3):
         gown[j] = gown[j] + grecv[j]
-    edge_up = remote(gown.at[0], gedge.at[1], e_send.at[0], e_recv.at[1], up)
-    edge_down = remote(gown.at[2], gedge.at[0], e_send.at[1], e_recv.at[0], down)
-    pl.when(has_up)(edge_up.start)
-    pl.when(has_down)(edge_down.start)
+    edge_far = remote(gown.at[fj], gedge.at[0], e_send.at[0], e_recv.at[0], {"row": behind})
+    edge_near = remote(gown.at[pj], gedge.at[1], e_send.at[1], e_recv.at[1], pair)
+    pl.when(has_behind)(edge_far.start)
 
     for p in range(1, modes // 2):
         start_scatter(p)
+
+    @pl.when(has_ahead)
+    def _():
+        edge_far.wait_recv()
+        gown[pj] = gown[pj] + gedge[0]
+
+    edge_near.start()
 
     def gather(p, hop):
         to = lax.rem(me + hop, rows)
@@ -292,19 +329,9 @@
             row_slice(red, p, me)[...] = red_chunk
             each_peer(rows, lambda hop: gather(p, hop).start())
 
-    @pl.when(jnp.logical_not(has_up))
-    def _():
-        gedge[0] = zero
-
-    @pl.when(jnp.logical_not(has_down))
-    def _():
-        gedge[1] = zero
-
-    pl.when(has_up)(edge_down.wait_recv)
-    pl.when(has_down)(edge_up.wait_recv)
-    for q in range(2):
-        grad = gown[1, q] + gedge[0, q] + gedge[1, q]
-        obj_out[q] = obj_ref[q] - object_rate * grad / weight
+    edge_near.wait_recv()
+    for q in range(2):
+        obj_out[q] = object_rate * (gown[1, q] + gedge[1, q]) / weight
 
     def swap(p):
         return remote(red.at[p], red_other.at[p], o_send.at[p], o_recv.at[p], mate)
@@ -319,26 +346,21 @@
         swap(p).start()
         k = 2 * p + col
         for q in range(2):
-            probe_out[k, q] = probe_ref[k, q] - probe_rate * red[p, q * n : (q + 1) * n] / tiles
+            probe_out[k, q] = probe_rate * red[p, q * n : (q + 1) * n] / tiles
     for p in range(modes // 2):
         swap(p).wait()
         k = 2 * p + 1 - col
         for q in range(2):
-            probe_out[k, q] = probe_ref[k, q] - probe_rate * red_other[p, q * n : (q + 1) * n] / tiles
+            probe_out[k, q] = probe_rate * red_other[p, q * n : (q + 1) * n] / tiles
 
     to_mate.wait_send()
-
-    @pl.when(has_up)
-    def _():
-        to_up.wait_send()
-        relay_up.wait_send()
-        edge_up.wait_send()
-
-    @pl.when(has_down)
-    def _():
-        to_down.wait_send()
-        relay_down.wait_send()
-        edge_down.wait_send()
+    edge_near.wait_send()
+    pl.when(has_behind)(edge_far.wait_send)
+    for q in range(2):
+        swaps[q].wait_send()
+        relays[q].wait_send()
+        pl.when(has_ahead)(hops[q].wait_send)
+        pl.when(has_behind)(passes[q].wait_send)
 
     for p in range(modes // 2):
 
@@ -348,6 +370,11 @@
             pl.when(me < owners)(gather(p, hop).wait_send)
 
         each_peer(rows, drain)
+
+
+def finish(obj_ref, probe_ref, obj_step, probe_step, obj_out, probe_out):
+    obj_out[...] = obj_ref[...] - obj_step[...]
+    probe_out[...] = probe_ref[...] - probe_step[...]
 
 
 def body(rows, object_field, probe, patterns, offsets, counts):
@@ -360,7 +387,7 @@
     smem = pl.BlockSpec(memory_space=pltpu.SMEM)
     dma = pltpu.SemaphoreType.DMA
     wide, tall = (slots, 2 * n, modes * n), (slots, modes * n, 2 * n)
-    return pl.pallas_call(
+    steps = pl.pallas_call(
         functools.partial(kernel, rows, modes, slots, n, owners),
         out_shape=(
             jax.ShapeDtypeStruct(object_field.shape, F32),
@@ -389,13 +416,22 @@
             pltpu.VMEM((pairs, rows, 2 * n // owners, n), F32),
             pltpu.VMEM((pairs, 2 * n, n), F32),
             pltpu.VMEM((pairs, 2 * n, n), F32),
-            dma((5,)), dma((5,)), dma((1,)), dma((1,)), dma((2,)), dma((2,)),
+            dma((9,)), dma((9,)), dma((1,)), dma((1,)), dma((2,)), dma((2,)),
             dma((pairs,)), dma((pairs,)),
             dma((pairs, rows)), dma((pairs, rows)), dma((pairs, rows)), dma((pairs, rows)),
-            dma((pairs,)), dma((pairs,)),
+            dma((pairs,)), dma((pairs,)), pltpu.SemaphoreType.REGULAR((max(1, rows.bit_length()),)),
         ],
         compiler_params=pltpu.CompilerParams(collective_id=0, has_side_effects=True),
     )(offsets, counts, object_field, probe, patterns, tables)
+    return pl.pallas_call(
+        finish,
+        out_shape=(
+            jax.ShapeDtypeStruct(object_field.shape, F32),
+            jax.ShapeDtypeStruct(probe.shape, F32),
+        ),
+        in_specs=[vmem] * 4,
+        out_specs=(vmem, vmem),
+    )(object_field, probe, *steps)
 
 
 def solution(mesh):

time: 42 us -> 41.4 us (0.986)
  local copies, waits for them, and re-layouts: 3.44 us -> 0 us
  Pallas kernels: 37 us -> 39.9 us
    unnamed x2 -> x0, local copies, waits for them, and re-layouts: 3.44 us -> none
    pallas_call x0 -> x1, Pallas kernels: none -> 2.14 us  [body(): pl.pallas_call(finish, out_shape=(jax.ShapeDtypeStruct(object_field.shape...]
    pallas_call x1, Pallas kernels: 37 us -> 37.8 us  [body(): pl.pallas_call(functools.partial(kernel, rows, modes, slots, n, owners),...]
where the time goes in v2:
time: 41.4 us; the launch traced here: 41.2 us
  Pallas kernels  39.9 us (96%)
  between operations  1.28 us (3%)
    pallas_call x1, Pallas kernels, body(): pl.pallas_call(functools.partial(kernel, rows, modes, slots, n, owners),...  37.8 us
    pallas_call x1, Pallas kernels, body(): pl.pallas_call(finish, out_shape=(jax.ShapeDtypeStruct(object_field.shape...  2.14 us

profile of v2, /device:TPU:0, one launch (start us, length us, event | category | flops | bytes accessed | tf_op | source)
XLA Modules:
  0.0 41.2 jit_solution(4703016102990702969)
XLA Ops:
  1.3 37.8 %shard_map.77 = (f32[2,128,128]{2,1,0:T(8,128)}, f32[4,2,128,128]{3,2,1,0:T(8,128)}) custom-call(s32[1,1,2,2]{3,2,1,0:T(2,128)} %off_ref.1, s32[1,1]{1,0:T(1,128)S(6)} %copy.8.cnt_ref, f32[2,128,128]{2,1,0:T(8,128)} %obj_ref.3, f32[4,2,128,128]{3,2,1,0:T(8,128)} %probe_ref.3, f32[1,1,2,128,128]{4,3,2,1,0:T(8,128)} %pat_ref.1, ...), custom_call_target="tpu_custom_call" | custom-call | tf_op jit(solution)/shard_map/pallas_call | solution.py:390
  39.1 2.1 %shard_map.78 = (f32[2,128,128]{2,1,0:T(8,128)}, f32[4,2,128,128]{3,2,1,0:T(8,128)}) custom-call(f32[2,128,128]{2,1,0:T(8,128)} %obj_ref.3, f32[4,2,128,128]{3,2,1,0:T(8,128)} %probe_ref.3, f32[2,128,128]{2,1,0:T(8,128)} %get-tuple-element.4.obj_step, f32[4,2,128,128]{3,2,1,0:T(8,128)} %get-tuple-element.5.probe_step), custom_call_target="tpu_custom_call" | custom-call | tf_op jit(solution)/shard_map/pallas_call | solution.py:426

commit v3 on v1

--- a/solution.py
+++ b/solution.py
@@ -57,7 +57,7 @@
     frame, xh, xl, yh, yl, far, vh, vl, win, gacc,
     gown, gpar, grecv, gedge, term, tpart, acc, pieces, red, red_other,
     h_send, h_recv, g_send, g_recv, e_send, e_recv, t_send, t_recv,
-    rs_send, rs_recv, ag_send, ag_recv, o_send, o_recv,
+    rs_send, rs_recv, ag_send, ag_recv, o_send, o_recv, news,
 ):
     me = lax.axis_index("row")
     col = lax.axis_index("col")
@@ -69,15 +69,35 @@
     has_up, has_down = me > 0, me < rows - 1
     chunk = 2 * n // owners
 
+    def if_row(row, act):
+        pl.when(jnp.logical_and(row >= 0, row < rows))(lambda: act({"row": row}))
+
+    def present(distance):
+        return (me >= distance).astype(jnp.int32) + (me + distance < rows).astype(jnp.int32)
+
     barrier = pltpu.get_barrier_semaphore()
-    pl.semaphore_signal(barrier, inc=1, device_id=mate, device_id_type=MESH)
-
-    def greet(hop):
-        other = lax.rem(me + hop, rows)
-        pl.semaphore_signal(barrier, inc=1, device_id={"row": other}, device_id_type=MESH)
-
-    each_peer(rows, greet)
-    pl.semaphore_wait(barrier, rows)
+
+    def greet(to):
+        pl.semaphore_signal(barrier, inc=1, device_id=to, device_id_type=MESH)
+
+    if_row(me + 1, greet)
+    if_row(me - 1, greet)
+    greet(mate)
+    pl.semaphore_wait(barrier, 1 + present(1))
+
+    rounds = [2]
+    while 2 * rounds[-1] < rows:
+        rounds.append(2 * rounds[-1])
+
+    def tell(r):
+        def act(to):
+            pl.semaphore_signal(news.at[r], inc=1, device_id=to, device_id_type=MESH)
+
+        if_row(me - rounds[r], act)
+        if_row(me + rounds[r], act)
+
+    def hear(r):
+        pl.semaphore_wait(news.at[r], present(rounds[r]))
 
     def remote(src, dst, send, recv, to):
         return pltpu.make_async_remote_copy(
@@ -128,6 +148,8 @@
     to_mate.wait_recv()
     pl.when(has_up)(relay_up.wait_recv)
     pl.when(has_down)(relay_down.wait_recv)
+
+    tell(0)
 
     r_hi, r_lo, l_hi, l_lo = (tab_ref.at[t] for t in range(4))
     row_id = lax.broadcasted_iota(jnp.int32, (n, n), 0)
@@ -178,6 +200,10 @@
                 yh[spot] = hi
                 yl[spot] = lo
 
+    for r in range(1, len(rounds)):
+        hear(r - 1)
+        tell(r)
+
     def to_partner(p):
         return remote(term.at[2 * p + 1 - col], tpart.at[p], t_send.at[p], t_recv.at[p], mate)
 
@@ -210,6 +236,31 @@
                     term[k, 0], term[k, 1] = term[k, 0] + tr, term[k, 1] + ti
         to_partner(p).start()
 
+    def row_slice(ref, p, owner):
+        return ref.at[p, pl.ds(pl.multiple_of(owner * chunk, 8), chunk)]
+
+    def scatter(p, hop):
+        to = lax.rem(me + hop, rows)
+        src = lax.rem(me + rows - hop, rows)
+        return (
+            to,
+            remote(row_slice(acc, p, to), pieces.at[p, hop], rs_send.at[p, hop], rs_recv.at[p, hop], {"row": to}),
+        )
+
+    def start_scatter(p):
+        to_partner(p).wait()
+        for q in range(2):
+            acc[p, q * n : (q + 1) * n] = term[2 * p + col, q] + tpart[p, q]
+
+        def step(hop):
+            to, copy = scatter(p, hop)
+            pl.when(to < owners)(copy.start)
+
+        each_peer(rows, step)
+
+    hear(len(rounds) - 1)
+    start_scatter(0)
+
     for q in range(2):
         own = [jnp.zeros((n, n), F32)] * 3
         par = [jnp.zeros((n, n), F32)] * 3
@@ -232,29 +283,9 @@
     across = remote(gpar, grecv, g_send.at[0], g_recv.at[0], mate)
     across.start()
 
-    def row_slice(ref, p, owner):
-        return ref.at[p, pl.ds(pl.multiple_of(owner * chunk, 8), chunk)]
-
-    def scatter(p, hop):
-        to = lax.rem(me + hop, rows)
-        src = lax.rem(me + rows - hop, rows)
-        return (
-            to,
-            remote(row_slice(acc, p, to), pieces.at[p, hop], rs_send.at[p, hop], rs_recv.at[p, hop], {"row": to}),
-        )
-
-    def start_scatter(p):
-        to_partner(p).wait()
-        for q in range(2):
-            acc[p, q * n : (q + 1) * n] = term[2 * p + col, q] + tpart[p, q]
-
-        def step(hop):
-            to, copy = scatter(p, hop)
-            pl.when(to < owners)(copy.start)
-
-        each_peer(rows, step)
-
-    start_scatter(0)
+
+    for p in range(1, modes // 2):
+        start_scatter(p)
 
     across.wait()
     for j in range(3):
@@ -264,9 +295,6 @@
     pl.when(has_up)(edge_up.start)
     pl.when(has_down)(edge_down.start)
 
-    for p in range(1, modes // 2):
-        start_scatter(p)
-
     def gather(p, hop):
         to = lax.rem(me + hop, rows)
         here = row_slice(red, p, me)
@@ -304,7 +332,7 @@
     pl.when(has_down)(edge_up.wait_recv)
     for q in range(2):
         grad = gown[1, q] + gedge[0, q] + gedge[1, q]
-        obj_out[q] = obj_ref[q] - object_rate * grad / weight
+        obj_out[q] = object_rate * grad / weight
 
     def swap(p):
         return remote(red.at[p], red_other.at[p], o_send.at[p], o_recv.at[p], mate)
@@ -319,12 +347,12 @@
         swap(p).start()
         k = 2 * p + col
         for q in range(2):
-            probe_out[k, q] = probe_ref[k, q] - probe_rate * red[p, q * n : (q + 1) * n] / tiles
+            probe_out[k, q] = probe_rate * red[p, q * n : (q + 1) * n] / tiles
     for p in range(modes // 2):
         swap(p).wait()
         k = 2 * p + 1 - col
         for q in range(2):
-            probe_out[k, q] = probe_ref[k, q] - probe_rate * red_other[p, q * n : (q + 1) * n] / tiles
+            probe_out[k, q] = probe_rate * red_other[p, q * n : (q + 1) * n] / tiles
 
     to_mate.wait_send()
 
@@ -348,6 +376,11 @@
             pl.when(me < owners)(gather(p, hop).wait_send)
 
         each_peer(rows, drain)
+
+
+def finish(obj_ref, probe_ref, obj_step, probe_step, obj_out, probe_out):
+    obj_out[...] = obj_ref[...] - obj_step[...]
+    probe_out[...] = probe_ref[...] - probe_step[...]
 
 
 def body(rows, object_field, probe, patterns, offsets, counts):
@@ -360,7 +393,7 @@
     smem = pl.BlockSpec(memory_space=pltpu.SMEM)
     dma = pltpu.SemaphoreType.DMA
     wide, tall = (slots, 2 * n, modes * n), (slots, modes * n, 2 * n)
-    return pl.pallas_call(
+    steps = pl.pallas_call(
         functools.partial(kernel, rows, modes, slots, n, owners),
         out_shape=(
             jax.ShapeDtypeStruct(object_field.shape, F32),
@@ -392,10 +425,19 @@
             dma((5,)), dma((5,)), dma((1,)), dma((1,)), dma((2,)), dma((2,)),
             dma((pairs,)), dma((pairs,)),
             dma((pairs, rows)), dma((pairs, rows)), dma((pairs, rows)), dma((pairs, rows)),
-            dma((pairs,)), dma((pairs,)),
+            dma((pairs,)), dma((pairs,)), pltpu.SemaphoreType.REGULAR((max(1, rows.bit_length()),)),
         ],
         compiler_params=pltpu.CompilerParams(collective_id=0, has_side_effects=True),
     )(offsets, counts, object_field, probe, patterns, tables)
+    return pl.pallas_call(
+        finish,
+        out_shape=(
+            jax.ShapeDtypeStruct(object_field.shape, F32),
+            jax.ShapeDtypeStruct(probe.shape, F32),
+        ),
+        in_specs=[vmem] * 4,
+        out_specs=(vmem, vmem),
+    )(object_field, probe, *steps)
 
 
 def solution(mesh):

time: 42 us -> 40 us (0.952)
  local copies, waits for them, and re-layouts: 3.44 us -> 0 us
  Pallas kernels: 37 us -> 38.6 us
    unnamed x2 -> x0, local copies, waits for them, and re-layouts: 3.44 us -> none
    pallas_call x0 -> x1, Pallas kernels: none -> 2.14 us  [body(): pl.pallas_call(finish, out_shape=(jax.ShapeDtypeStruct(object_field.shape...]
    pallas_call x1, Pallas kernels: 37 us -> 36.4 us  [body(): pl.pallas_call(functools.partial(kernel, rows, modes, slots, n, owners),...]
where the time goes in v3:
time: 40 us; the launch traced here: 39.9 us
  Pallas kernels  38.6 us (96%)
  between operations  1.28 us (3%)
    pallas_call x1, Pallas kernels, body(): pl.pallas_call(functools.partial(kernel, rows, modes, slots, n, owners),...  36.4 us
    pallas_call x1, Pallas kernels, body(): pl.pallas_call(finish, out_shape=(jax.ShapeDtypeStruct(object_field.shape...  2.14 us

profile of v3, /device:TPU:0, one launch (start us, length us, event | category | flops | bytes accessed | tf_op | source)
XLA Modules:
  0.0 39.9 jit_solution(410661510106563803)
XLA Ops:
  1.3 36.4 %shard_map.77 = (f32[2,128,128]{2,1,0:T(8,128)}, f32[4,2,128,128]{3,2,1,0:T(8,128)}) custom-call(s32[1,1,2,2]{3,2,1,0:T(2,128)} %off_ref.1, s32[1,1]{1,0:T(1,128)S(6)} %copy.8.cnt_ref, f32[2,128,128]{2,1,0:T(8,128)} %obj_ref.3, f32[4,2,128,128]{3,2,1,0:T(8,128)} %probe_ref.3, f32[1,1,2,128,128]{4,3,2,1,0:T(8,128)} %pat_ref.1, ...), custom_call_target="tpu_custom_call" | custom-call | tf_op jit(solution)/shard_map/pallas_call | solution.py:396
  37.7 2.1 %shard_map.78 = (f32[2,128,128]{2,1,0:T(8,128)}, f32[4,2,128,128]{3,2,1,0:T(8,128)}) custom-call(f32[2,128,128]{2,1,0:T(8,128)} %obj_ref.3, f32[4,2,128,128]{3,2,1,0:T(8,128)} %probe_ref.3, f32[2,128,128]{2,1,0:T(8,128)} %get-tuple-element.4.obj_step, f32[4,2,128,128]{3,2,1,0:T(8,128)} %get-tuple-element.5.probe_step), custom_call_target="tpu_custom_call" | custom-call | tf_op jit(solution)/shard_map/pallas_call | solution.py:432
